TPU v7x, 32 devices: a whole 2x2x4 slice. The times are simulated.
32 devices in a mesh: grp: 1, exp: 32 (over z, y, x, core).
Axes of the slice: x: 2, y: 2, z: 4, core: 2. Of those that a mesh axis runs over, the one named last changes fastest.
Arguments:
- tokens: bfloat16 [512, 2048], P(('grp', 'exp')), may hold values from -6 to 6
- routed_expert_index: int32 [512, 6], P(('grp', 'exp')), may hold values from 0 to 15, all different within a row; in each aligned block of 16 rows (0 to 15, 16 to 31, ...) at most 8 rows name the same one
- routing_gate_weight: float32 [512, 6], P(('grp', 'exp')), may hold values from 0.05 to 0.5
- token_adapter_index: int32 [512], P('grp'), may hold values from 0 to 511
- gate_weight_pieces: bfloat16 [32, 2048, 704], P('exp'), may hold values from -0.125 to 0.125
- up_weight: bfloat16 [32, 2048, 704], P('exp'), may hold values from -0.125 to 0.125
- down_weight: bfloat16 [32, 704, 2048], P('exp'), may hold values from -0.15625 to 0.15625
- adapter_down_matrix: bfloat16 [2048, 8192], P('exp'), may hold values from -0.125 to 0.125
- adapter_up_matrix: bfloat16 [2048, 8192], P('exp'), may hold values from -1.5 to 1.5
Outputs:
- mixed: bfloat16 [512, 2048], P(('grp', 'exp'))
Inputs may be any that keep to these rules, and one draw needn't show every extreme that they name: `routed_expert_index`: each token names 6 different experts; among the 16 tokens of one index of exp (aligned blocks of rows) no expert is named more than 8 times.
All inputs are finite; a program needn't handle non-finite values.
Results may differ from a plain program's by a relative error of at most 0.009.
Values may be sent and summed in bfloat16 or wider, within the bound.
A program may use at most 128 MiB of HBM per device.

v0:
```python
import functools

import jax
import jax.numpy as jnp
from jax import lax
from jax.experimental import pallas as pl
from jax.experimental.pallas import tpu as pltpu
from jax.sharding import PartitionSpec as P

RANK = 16
LANES = 128
BF16 = jnp.bfloat16
F32 = jnp.float32
MESH = pl.DeviceIdType.MESH


def dot_nt(a, b):
    return lax.dot_general(a, b, (((1,), (1,)), ((), ())), preferred_element_type=F32)


def kernel(
    chips, cap, top, x_ref, idx_ref, gate_ref, aid_ref, wg_hbm, wu_hbm, wd_hbm, adn_hbm, aup_hbm, out_ref,
    wg, wu, wd, adn, aup, col, disp, recv_a, recv_b, xs, hid, y_own, sib_send, sib_recv,
    rs_send, rs_recv, ag, cor_send, cor_recv, ret_send, ret_recv, low,
    w_sem, adl_sem, ad_s, ad_r, col_s, col_r, disp_s, disp_r, fwd_s, fwd_r, rs_s, rs_r,
    ag_s, ag_r, cor_s, cor_r, ret_s, ret_r, sib_s, sib_r,
):
    me = lax.axis_index("exp")
    q = lax.div(me, 2)
    c = lax.rem(me, 2)
    sib = me + 1 - 2 * c
    rows, width = x_ref.shape
    feats = adn_hbm.shape[0]
    bank = adn_hbm.shape[1]
    group = chips * rows
    slots = chips * cap
    parts, wide_n = y_own.shape[0], y_own.shape[2]
    off = pl.multiple_of(lax.rem(me * feats, LANES), feats)

    def remote(src, dst, ss, rs, dev):
        return pltpu.make_async_remote_copy(
            src_ref=src, dst_ref=dst, send_sem=ss, recv_sem=rs, device_id={"exp": dev}, device_id_type=MESH
        )

    def peer(r):
        return lax.rem(q + r, chips)

    def source(r):
        return lax.rem(q + chips - r, chips)

    def others(fn, first=1, last=chips):
        def step(r, carry):
            fn(r)
            return carry

        lax.fori_loop(first, last, step, 0)

    barrier = pltpu.get_barrier_semaphore()
    if 2 * feats < LANES:
        adn[...] = jnp.zeros_like(adn)
        aup[...] = jnp.zeros_like(aup)
    others(lambda r: pl.semaphore_signal(barrier, inc=1, device_id={"exp": 2 * peer(r) + c}, device_id_type=MESH))
    pl.semaphore_signal(barrier, inc=1, device_id={"exp": sib}, device_id_type=MESH)

    own_rows = pl.ds(off, feats)
    local = [
        pltpu.make_async_copy(adn_hbm, adn.at[own_rows], adl_sem.at[0]),
        pltpu.make_async_copy(wg_hbm.at[0], wg, w_sem.at[0]),
        pltpu.make_async_copy(wu_hbm.at[0], wu, w_sem.at[1]),
        pltpu.make_async_copy(aup_hbm, aup.at[own_rows], adl_sem.at[1]),
        pltpu.make_async_copy(wd_hbm.at[0], wd, w_sem.at[2]),
    ]
    for cp in local:
        cp.start()

    slot = lax.broadcasted_iota(jnp.int32, (slots, rows), 0)
    slot_e = lax.div(slot, cap)
    chosen = jnp.zeros((slots, rows), F32)
    weight = jnp.zeros((slots, rows), F32)
    for k in range(top):
        hit = idx_ref[k : k + 1, :] == slot_e
        chosen = chosen + jnp.where(hit, 1.0, 0.0)
        weight = weight + jnp.where(hit, gate_ref[k : k + 1, :], 0.0)
    earlier = jnp.where(
        lax.broadcasted_iota(jnp.int32, (rows, rows), 0) < lax.broadcasted_iota(jnp.int32, (rows, rows), 1), 1.0, 0.0
    )
    rank_of = jnp.dot(chosen.astype(BF16), earlier.astype(BF16), preferred_element_type=F32)
    slot_p = lax.rem(slot, cap).astype(F32)
    pick = jnp.where((chosen > 0.5) & (rank_of == slot_p), 1.0, 0.0)
    packed = jnp.dot(pick.astype(BF16), x_ref[...], preferred_element_type=F32)
    disp[...] = packed.reshape(chips, cap, width).astype(BF16)
    recv_a[pl.ds(q, 1)] = disp[pl.ds(q, 1)]

    def lanes_of(chip):
        return pl.ds(pl.multiple_of(lax.div(chip * 2 * feats, LANES) * LANES, LANES), LANES)

    col[pl.ds(q, 1)] = x_ref[:, lanes_of(q)].reshape(1, rows, LANES)

    pl.semaphore_wait(barrier, chips)

    def col_copy(to, slot):
        return remote(x_ref.at[:, lanes_of(to)], col.at[slot], col_s.at[to], col_r.at[slot], 2 * to + c)

    def disp_copy(to, slot):
        return remote(disp.at[to], recv_a.at[slot], disp_s.at[to], disp_r.at[slot], 2 * to + c)

    def fwd_copy(block):
        return remote(recv_a.at[block], recv_b.at[block], fwd_s.at[block], fwd_r.at[block], sib)

    def rs_copy(to, slot):
        return remote(rs_send.at[to], rs_recv.at[slot], rs_s.at[to], rs_r.at[slot], 2 * to + c)

    def ag_copy(to, slot):
        return remote(low, ag.at[slot], ag_s.at[to], ag_r.at[slot], 2 * to + c)

    def cor_copy(to, slot):
        return remote(cor_send.at[to], cor_recv.at[slot], cor_s.at[to], cor_r.at[slot], 2 * to + c)

    def ret_copy(j, to, slot):
        return remote(
            ret_send.at[j, to], ret_recv.at[j, slot], ret_s.at[j * chips + to], ret_r.at[j * chips + slot], 2 * to + c
        )

    def sib_copy(j):
        return remote(sib_send.at[j], sib_recv.at[j], sib_s.at[j], sib_r.at[j], sib)

    others(lambda r: col_copy(peer(r), q).start())
    adn_copy = remote(adn_hbm, adn.at[own_rows], ad_s.at[0], ad_r.at[0], sib)
    aup_copy = remote(aup_hbm, aup.at[own_rows], ad_s.at[1], ad_r.at[1], sib)
    adn_copy.start()
    early = 1 + (chips - 1) * 5 // 8
    others(lambda r: disp_copy(peer(r), q).start(), 1, early)
    aup_copy.start()
    fwd_copy(q).start()

    piece = 8 * LANES // (2 * rows)
    ids = []
    for first in range(0, chips, piece):
        n = min(piece, chips - first)
        part = lax.broadcasted_iota(jnp.int32, (n * rows, n * 2 * rows), 1)
        row = lax.broadcasted_iota(jnp.int32, (n * rows, n * 2 * rows), 0)
        here = lax.div(row, rows) * (2 * rows) + lax.rem(row, rows) + c * rows
        values = aid_ref[:, first * 2 * rows : (first + n) * 2 * rows].astype(F32)
        ids.append(jnp.sum(jnp.where(part == here, values, 0.0), axis=1, keepdims=True))
    ids = jnp.concatenate(ids, axis=0) if len(ids) > 1 else ids[0]
    ids = jnp.broadcast_to(ids, (group, LANES)).astype(jnp.int32)
    per = LANES // RANK
    id_hi = lax.div(ids, per)
    id_lo = ids - id_hi * per
    lane_g = lax.broadcasted_iota(jnp.int32, (group, LANES), 1)
    keep = lax.div(lane_g, RANK) == id_lo

    others(lambda r: col_copy(q, source(r)).wait_recv())
    local[0].wait()
    adn_copy.wait_recv()
    cols = col[...].reshape(group, LANES)
    span = 512
    sub = span // LANES

    def down_step(i, acc):
        at = pl.multiple_of(i * span, span)
        h = jnp.dot(cols, adn[:, pl.ds(at, span)], preferred_element_type=F32)
        for s in range(sub):
            acc = jnp.where(id_hi == i * sub + s, h[:, s * LANES : (s + 1) * LANES], acc)
        return acc

    terms = lax.fori_loop(0, bank // span, down_step, jnp.zeros((group, LANES), F32))
    terms = jnp.where(keep, terms, 0.0).astype(BF16)
    fi = lax.broadcasted_iota(jnp.int32, (LANES, LANES), 0)
    fj = lax.broadcasted_iota(jnp.int32, (LANES, LANES), 1)
    fold = jnp.where(lax.rem(fi, RANK) == lax.rem(fj, RANK), 1.0, 0.0).astype(BF16)
    turn = lax.div(lane_g, RANK) == lax.rem(lax.broadcasted_iota(jnp.int32, (group, LANES), 0), per)
    folded = jnp.where(turn, jnp.dot(terms, fold, preferred_element_type=F32), 0.0)
    rs_send[...] = jnp.sum(folded.reshape(group // per, per, LANES), axis=1).reshape(chips, rows // per, LANES)
    rs_recv[pl.ds(q, 1)] = rs_send[pl.ds(q, 1)]
    others(lambda r: rs_copy(peer(r), q).start())

    others(lambda r: disp_copy(peer(r), q).start(), early, chips)

    def forward(r):
        disp_copy(q, source(r)).wait_recv()
        fwd_copy(source(r)).start()

    others(forward, 1, early)
    others(lambda r: rs_copy(q, source(r)).wait_recv())
    low[...] = jnp.sum(rs_recv[...], axis=0).astype(BF16).astype(F32)
    ag[pl.ds(q, 1)] = low[...].reshape(1, rows // per, LANES)
    others(lambda r: ag_copy(peer(r), q).start())
    others(forward, early, chips)

    half = wd.shape[0]
    xs[:slots] = recv_a[...].astype(F32).reshape(slots, width).astype(BF16)
    local[1].wait()
    local[2].wait()
    local[4].wait()
    fwd_copy(q).wait_recv()
    others(lambda r: fwd_copy(source(r)).wait_recv())
    xs[slots:] = recv_b[...].astype(F32).reshape(slots, width).astype(BF16)
    cut = -(-half // (2 * LANES)) * LANES
    for a, b in ((0, cut), (cut, half)):
        g = dot_nt(wg[a:b], xs[...])
        u = dot_nt(wu[a:b], xs[...])
        hid[:, a:b] = (g / (1.0 + jnp.exp(-g)) * u).T.astype(BF16)

    def finish(j):
        sib_copy(j).wait_recv()
        ret_send[j] = (y_own[j].reshape(chips, cap, wide_n) + sib_recv[j].astype(F32)).astype(BF16)
        ret_recv[j, pl.ds(q, 1)] = ret_send[j, pl.ds(q, 1)]
        others(lambda r: ret_copy(j, peer(r), q).start())

    for j in range(parts):
        y = jnp.dot(hid[...], wd[:, j * wide_n : (j + 1) * wide_n], preferred_element_type=F32)
        sib_send[j] = y[slots:].reshape(chips, cap, wide_n).astype(BF16)
        sib_copy(j).start()
        y_own[j] = y[:slots]
        if j > 0:
            finish(j - 1)
    finish(parts - 1)

    others(lambda r: ag_copy(q, source(r)).wait_recv())
    local[3].wait()
    aup_copy.wait_recv()
    ranks = jnp.broadcast_to(ag[...].reshape(group // per, 1, LANES), (group // per, per, LANES)).reshape(group, LANES)
    ranks = jnp.where(turn, ranks, 0.0).astype(BF16)
    ranks = jnp.where(keep, jnp.dot(ranks, fold, preferred_element_type=F32), 0.0)

    def up_step(i, acc):
        at = pl.multiple_of(i * span, span)
        wide = jnp.concatenate([jnp.where(id_hi == i * sub + s, ranks, 0.0).astype(BF16) for s in range(sub)], axis=1)
        return acc + dot_nt(wide, aup[:, pl.ds(at, span)])

    corr = lax.fori_loop(0, bank // span, up_step, jnp.zeros((group, LANES), F32))
    cor_send[...] = corr.astype(BF16).reshape(chips, rows, LANES)
    cor_recv[pl.ds(q, 1)] = cor_send[pl.ds(q, 1)]
    others(lambda r: cor_copy(peer(r), q).start())

    others(lambda r: cor_copy(q, source(r)).wait_recv())
    combine = (pick * weight).T
    c_hi = combine.astype(BF16)
    c_lo = (combine - c_hi.astype(F32)).astype(BF16)
    share = LANES // (2 * feats)
    for j in range(parts):
        others(lambda r: ret_copy(j, q, source(r)).wait_recv())
        back = ret_recv[j].astype(F32).reshape(slots, wide_n).astype(BF16)
        routed = jnp.dot(c_hi, back, preferred_element_type=F32) + jnp.dot(c_lo, back, preferred_element_type=F32)
        for i in range(wide_n // LANES):
            first = (j * wide_n // LANES + i) * share
            delta = cor_recv[first].astype(F32)
            for s in range(1, share):
                delta = delta + cor_recv[first + s].astype(F32)
            out_ref[:, j * wide_n + i * LANES : j * wide_n + (i + 1) * LANES] = (
                routed[:, i * LANES : (i + 1) * LANES] + delta
            ).astype(BF16)

    adn_copy.wait_send()
    aup_copy.wait_send()
    for j in range(parts):
        sib_copy(j).wait_send()
    fwd_copy(q).wait_send()

    def drain(r):
        to = peer(r)
        for cp in (col_copy, disp_copy, rs_copy, ag_copy, cor_copy):
            cp(to, q).wait_send()
        for j in range(parts):
            ret_copy(j, to, q).wait_send()
        fwd_copy(source(r)).wait_send()

    others(drain)


def per_device(tokens, idx, gates, aid, wg, wu, wd, adn, aup):
    devices = lax.axis_size("exp")
    chips = devices // 2
    rows, width = tokens.shape
    top = idx.shape[1]
    half = wd.shape[1]
    feats, bank = adn.shape
    need = 2 * (rows * top // devices + 1)
    cap = -(-need // 8) * 8
    slots = chips * cap
    short = rows * RANK // LANES
    parts = 4
    wide_n = width // parts
    blocks = lambda *s: pltpu.VMEM(s, BF16)
    sems = lambda n: pltpu.SemaphoreType.DMA((n,))
    vm = pl.BlockSpec(memory_space=pltpu.VMEM)
    hbm = pl.BlockSpec(memory_space=pl.ANY)
    return pl.pallas_call(
        functools.partial(kernel, chips, cap, top),
        out_shape=jax.ShapeDtypeStruct((rows, width), BF16),
        in_specs=[vm, vm, vm, vm, hbm, hbm, hbm, hbm, hbm],
        out_specs=vm,
        scratch_shapes=[
            blocks(half, width), blocks(half, width), blocks(half, width),
            blocks(LANES, bank), blocks(LANES, bank),
            blocks(chips, rows, LANES),
            blocks(chips, cap, width), blocks(chips, cap, width), blocks(chips, cap, width),
            blocks(2 * slots, width), blocks(2 * slots, half), pltpu.VMEM((parts, slots, wide_n), F32),
            blocks(parts, chips, cap, wide_n), blocks(parts, chips, cap, wide_n),
            pltpu.VMEM((chips, short, LANES), F32), pltpu.VMEM((chips, short, LANES), F32),
            pltpu.VMEM((chips, short, LANES), F32),
            blocks(chips, rows, LANES), blocks(chips, rows, LANES),
            blocks(parts, chips, cap, wide_n), blocks(parts, chips, cap, wide_n), pltpu.VMEM((short, LANES), F32),
            sems(3), sems(2), sems(2), sems(2),
            *[sems(chips) for _ in range(12)],
            sems(parts * chips), sems(parts * chips), sems(parts), sems(parts),
        ],
        compiler_params=pltpu.CompilerParams(
            collective_id=0, has_side_effects=True, vmem_limit_bytes=60 * 1024 * 1024
        ),
    )(tokens, idx.T, gates.T, aid.reshape(1, -1), wg.swapaxes(1, 2), wu.swapaxes(1, 2), wd, adn, aup)


def solution(mesh):
    placed = (
        P(("grp", "exp"), None),
        P(("grp", "exp"), None),
        P(("grp", "exp"), None),
        P("grp"),
        P("exp", None, None),
        P("exp", None, None),
        P("exp", None, None),
        P("exp", None),
        P("exp", None),
    )
    return jax.shard_map(
        per_device, mesh=mesh, in_specs=placed, out_specs=P(("grp", "exp"), None), check_vma=False
    )
```

profile of v0, /device:TPU:0, one launch (start us, length us, event | category | flops | bytes accessed | tf_op | source)
XLA Modules:
  0.0 48.9 jit_solution(17272089415678940711)
XLA Ops:
  0.0 47.4 %shard_map.91 = bf16[16,2048]{1,0:T(8,128)(2,1)} custom-call(bf16[16,2048]{1,0:T(8,128)(2,1)} %x_ref.1, s32[6,16]{1,0:T(8,128)} %bitcast.7, f32[6,16]{1,0:T(8,128)} %bitcast.8, s32[1,512]{1,0:T(1,128)} %bitcast.9, bf16[1,704,2048]{2,1,0:T(8,128)(2,1)} %bitcast.5, bf16[1,704,2048]{2,1,0:T(8,128)(2,1)} %bitcast.6, bf16[1,704,2048]{2,1,0:T(8,128)(2,1)} %wd_hbm.1, ...), custom_call_target="tpu_custom_call" | custom-call | tf_op jit(solution)/shard_map/pallas_call | solution.py:289
  47.4 1.5 %copy.11 = bf16[16,2048]{1,0:T(8,128)(2,1)} copy(bf16[16,2048]{1,0:T(8,128)(2,1)} %shard_map.91) | data formatting | bytes 131072
where the time goes:
time: 49.1 us; the launch traced here: 48.9 us
  Pallas kernels  47.4 us (97%)
  local copies, waits for them, and re-layouts  1.47 us (3%)
    pallas_call x1, Pallas kernels, per_device(): pl.pallas_call(functools.partial(kernel, chips, cap, top), out_shape=jax....  47.4 us
    unnamed x1, local copies, waits for them, and re-layouts  1.47 us

commit v1 on v0

v1 whole, which is shorter than its diff:
```python
import functools

import jax
import jax.numpy as jnp
from jax import lax
from jax.experimental import pallas as pl
from jax.experimental.pallas import tpu as pltpu
from jax.sharding import PartitionSpec as P

RANK = 16
LANES = 128
BF16 = jnp.bfloat16
F32 = jnp.float32
MESH = pl.DeviceIdType.MESH


def dot_nt(a, b):
    return lax.dot_general(a, b, (((1,), (1,)), ((), ())), preferred_element_type=F32)


def kernel(
    line, plane, cap, top, x_ref, idx_ref, gate_ref, aid_ref, wg_hbm, wu_hbm, wd_hbm, adn_hbm, aup_hbm, out_ref,
    wg, wu, wd, adn, aup, line_x, comb_send, line_comb, col, disp, recv_a, recv_b, xs, hid, y_own, sib_send, sib_recv,
    lr_send, lr1_recv, lr2_send, lr2_recv, cor_send, cor_recv, ret_send, ret_recv, part_send, part_recv, own_part,
    w_sem, adl_sem, ad_s, ad_r, x_s, x_r, cb_s, cb_r, col_s, col_r, disp_s, disp_r, fwd_s, fwd_r, l1_s, l1_r,
    l2_s, l2_r, cor_s, cor_r, ret_s, ret_r, part_s, part_r, sib_s, sib_r,
):
    me = lax.axis_index("exp")
    q = lax.div(me, 2)
    c = lax.rem(me, 2)
    z = lax.div(q, plane)
    g = lax.rem(q, plane)
    sib = me + 1 - 2 * c
    rows, width = x_ref.shape
    feats = adn_hbm.shape[0]
    bank = adn_hbm.shape[1]
    chips = line * plane
    group = chips * rows
    slots = chips * cap
    block = plane * cap
    wide_n = width // line
    off = pl.multiple_of(lax.rem(me * feats, LANES), feats)
    half_l = LANES // 2

    def remote(src, dst, ss, rs, dev):
        return pltpu.make_async_remote_copy(
            src_ref=src, dst_ref=dst, send_sem=ss, recv_sem=rs, device_id={"exp": dev}, device_id_type=MESH
        )

    def dev_z(to):
        return 2 * (to * plane + g) + c

    def dev_g(to):
        return 2 * (z * plane + to) + c

    side = lax.div(2 * z, line)
    mirror = side * z + (1 - side) * (line - 1 - z)

    def far(s):
        d = s + lax.div(s - mirror + line, line)
        return side * d + (1 - side) * (line - 1 - d)

    def loop(n, fn):
        def step(r, carry):
            fn(r)
            return carry

        lax.fori_loop(0, n, step, 0)

    def line_far(fn):
        loop(line - 1, lambda s: fn(far(s)))

    def line_near(fn):
        loop(line - 1, lambda s: fn(far(line - 2 - s)))

    def plane_peers(fn):
        loop(plane - 1, lambda r: fn(lax.rem(g + 1 + r, plane)))

    barrier = pltpu.get_barrier_semaphore()
    if 2 * feats < LANES:
        adn[...] = jnp.zeros_like(adn)
        aup[...] = jnp.zeros_like(aup)

    def greet(dev):
        pl.semaphore_signal(barrier, inc=1, device_id={"exp": dev}, device_id_type=MESH)

    line_far(lambda d: greet(dev_z(d)))
    plane_peers(lambda d: greet(dev_g(d)))
    greet(sib)

    own_rows = pl.ds(off, feats)
    local = [
        pltpu.make_async_copy(adn_hbm, adn.at[own_rows], adl_sem.at[0]),
        pltpu.make_async_copy(wg_hbm.at[0], wg, w_sem.at[0]),
        pltpu.make_async_copy(wu_hbm.at[0], wu, w_sem.at[1]),
        pltpu.make_async_copy(aup_hbm, aup.at[own_rows], adl_sem.at[1]),
        pltpu.make_async_copy(wd_hbm.at[0], wd, w_sem.at[2]),
    ]
    for cp in local:
        cp.start()

    slot = lax.broadcasted_iota(jnp.int32, (slots, rows), 0)
    slot_e = lax.div(slot, cap)
    chosen = jnp.zeros((slots, rows), F32)
    weight = jnp.zeros((slots, rows), F32)
    for k in range(top):
        hit = idx_ref[k : k + 1, :] == slot_e
        chosen = chosen + jnp.where(hit, 1.0, 0.0)
        weight = weight + jnp.where(hit, gate_ref[k : k + 1, :], 0.0)
    earlier = jnp.where(
        lax.broadcasted_iota(jnp.int32, (rows, rows), 0) < lax.broadcasted_iota(jnp.int32, (rows, rows), 1), 1.0, 0.0
    )
    rank_of = jnp.dot(chosen.astype(BF16), earlier.astype(BF16), preferred_element_type=F32)
    slot_p = lax.rem(slot, cap).astype(F32)
    combine = jnp.where((chosen > 0.5) & (rank_of == slot_p), weight, 0.0)
    for d in range(line):
        part = combine[d * block : (d + 1) * block].T
        hi = part.astype(BF16)
        lo = (part - hi.astype(F32)).astype(BF16)
        comb_send[d, :, :block] = hi
        comb_send[d, :, half_l : half_l + block] = lo
    line_comb[pl.ds(z, 1)] = comb_send[pl.ds(z, 1)]
    line_x[pl.ds(z, 1)] = x_ref[...].reshape(1, rows, width)

    pl.semaphore_wait(barrier, line + plane - 1)

    def lanes_of(chip):
        return pl.ds(pl.multiple_of(lax.div(chip * 2 * feats, LANES) * LANES, LANES), LANES)

    def chunk_of(i):
        return pl.ds(pl.multiple_of(i * wide_n, wide_n), wide_n)

    def x_copy(to, slot, i):
        return remote(
            x_ref.at[:, chunk_of(i)], line_x.at[slot, :, chunk_of(i)],
            x_s.at[to * line + i], x_r.at[slot * line + i], dev_z(to),
        )

    def comb_copy(to, slot):
        return remote(comb_send.at[to], line_comb.at[slot], cb_s.at[to], cb_r.at[slot], dev_z(to))

    def col_copy(to, slot, s):
        return remote(
            line_x.at[s, :, lanes_of(z * plane + to)], col.at[slot, s],
            col_s.at[to * line + s], col_r.at[slot * line + s], dev_g(to),
        )

    def disp_copy(to, slot, s):
        return remote(
            disp.at[to, s], recv_a.at[slot, s], disp_s.at[to * line + s], disp_r.at[slot * line + s], dev_g(to)
        )

    def fwd_copy(slot, s):
        at = slot * line + s
        return remote(recv_a.at[slot, s], recv_b.at[slot, s], fwd_s.at[at], fwd_r.at[at], sib)

    def lr1_copy(to, slot):
        return remote(lr_send, lr1_recv.at[slot], l1_s.at[to], l1_r.at[slot], dev_g(to))

    def lr2_copy(to, slot):
        return remote(lr2_send, lr2_recv.at[slot], l2_s.at[to], l2_r.at[slot], dev_z(to))

    def cor_copy(to, slot):
        return remote(cor_send.at[to], cor_recv.at[slot], cor_s.at[to], cor_r.at[slot], dev_g(to))

    def ret_copy(i, to, slot):
        return remote(
            ret_send.at[i, to], ret_recv.at[i, slot], ret_s.at[i * plane + to], ret_r.at[i * plane + slot], dev_g(to)
        )

    def turn_of(i, at):
        return lax.rem(at + 1 + i, line)

    def part_copy(i, to, slot, j):
        return remote(
            part_send.at[i, to], part_recv.at[slot, j], part_s.at[i * line + to], part_r.at[slot * line + j], dev_z(to)
        )

    def sib_copy(i):
        return remote(sib_send.at[i], sib_recv.at[i], sib_s.at[i], sib_r.at[i], sib)

    def send_x(i):
        line_far(lambda d: x_copy(d, z, lax.rem(d + i, line)).start())

    def own_col(s):
        col[pl.ds(g, 1), pl.ds(s, 1)] = line_x[pl.ds(s, 1), :, lanes_of(q)].reshape(1, 1, rows, LANES)

    send_x(0)
    plane_peers(lambda d: col_copy(d, g, z).start())
    line_far(lambda d: comb_copy(d, z).start())
    for i in range(1, line):
        send_x(i)
    adn_copy = remote(adn_hbm, adn.at[own_rows], ad_s.at[0], ad_r.at[0], sib)
    aup_copy = remote(aup_hbm, aup.at[own_rows], ad_s.at[1], ad_r.at[1], sib)
    adn_copy.start()

    def pack(s):
        pick = jnp.where(line_comb[s].astype(F32) > 0.0, 1.0, 0.0).T[:block].astype(BF16)
        packed = jnp.dot(pick, line_x[s], preferred_element_type=F32)
        disp[:, pl.ds(s, 1)] = packed.reshape(plane, 1, cap, width).astype(BF16)
        recv_a[pl.ds(g, 1), pl.ds(s, 1)] = disp[pl.ds(g, 1), pl.ds(s, 1)]
        plane_peers(lambda d: disp_copy(d, g, s).start())
        fwd_copy(g, s).start()

    pack(z)
    aup_copy.start()
    own_col(z)

    per = LANES // RANK
    ids = []
    near = line * rows
    for p in range(plane):
        lane = lax.broadcasted_iota(jnp.int32, (near, aid_ref.shape[1]), 1)
        row = lax.broadcasted_iota(jnp.int32, (near, aid_ref.shape[1]), 0)
        here = ((lax.div(row, rows) * plane + p) * 2 + c) * rows + lax.rem(row, rows)
        ids.append(jnp.sum(jnp.where(lane == here, aid_ref[...].astype(F32), 0.0), axis=1, keepdims=True))
    ids = jnp.broadcast_to(jnp.concatenate(ids, axis=0), (group, LANES)).astype(jnp.int32)
    id_hi = lax.div(ids, per)
    id_lo = ids - id_hi * per
    lane_g = lax.broadcasted_iota(jnp.int32, (group, LANES), 1)
    keep = lax.div(lane_g, RANK) == id_lo

    def relay_cols(s):
        x_copy(z, s, z).wait_recv()
        plane_peers(lambda d: col_copy(d, g, s).start())
        own_col(s)

    def relay_x(s):
        for i in range(1, line):
            x_copy(z, s, lax.rem(z + i, line)).wait_recv()
        comb_copy(z, s).wait_recv()
        pack(s)

    line_near(relay_cols)
    line_near(relay_x)

    plane_peers(lambda p: loop(line, lambda s: col_copy(g, p, s).wait_recv()))
    local[0].wait()
    adn_copy.wait_recv()
    cols = col[...].reshape(group, LANES)
    span = 512
    sub = span // LANES

    def down_step(i, acc):
        at = pl.multiple_of(i * span, span)
        h = jnp.dot(cols, adn[:, pl.ds(at, span)], preferred_element_type=F32)
        for s in range(sub):
            acc = jnp.where(id_hi == i * sub + s, h[:, s * LANES : (s + 1) * LANES], acc)
        return acc

    terms = lax.fori_loop(0, bank // span, down_step, jnp.zeros((group, LANES), F32))
    terms = jnp.where(keep, terms, 0.0).astype(BF16)
    fi = lax.broadcasted_iota(jnp.int32, (LANES, LANES), 0)
    fj = lax.broadcasted_iota(jnp.int32, (LANES, LANES), 1)
    fold = jnp.where(lax.rem(fi, RANK) == lax.rem(fj, RANK), 1.0, 0.0).astype(BF16)
    turn = lax.div(lane_g, RANK) == lax.rem(lax.broadcasted_iota(jnp.int32, (group, LANES), 0), per)
    folded = jnp.where(turn, jnp.dot(terms, fold, preferred_element_type=F32), 0.0)
    lr_send[...] = jnp.sum(folded.reshape(group // per, per, LANES), axis=1)
    lr1_recv[pl.ds(g, 1)] = lr_send[...].reshape(1, group // per, LANES)
    plane_peers(lambda d: lr1_copy(d, g).start())

    def forward(s):
        def one(p):
            disp_copy(g, p, s).wait_recv()
            fwd_copy(p, s).start()

        plane_peers(one)

    forward(z)
    plane_peers(lambda p: lr1_copy(g, p).wait_recv())
    lr2_send[...] = jnp.sum(lr1_recv[...], axis=0)
    lr2_recv[pl.ds(z, 1)] = lr2_send[...].reshape(1, group // per, LANES)
    line_far(lambda d: lr2_copy(d, z).start())
    line_near(forward)

    half = wd.shape[0]
    xs[:slots] = recv_a[...].astype(F32).reshape(slots, width).astype(BF16)
    local[1].wait()
    local[2].wait()
    local[4].wait()
    loop(plane, lambda p: loop(line, lambda s: fwd_copy(p, s).wait_recv()))
    xs[slots:] = recv_b[...].astype(F32).reshape(slots, width).astype(BF16)
    cut = -(-half // (2 * LANES)) * LANES
    for a, b in ((0, cut), (cut, half)):
        gt = dot_nt(wg[a:b], xs[...])
        up = dot_nt(wu[a:b], xs[...])
        hid[:, a:b] = (gt / (1.0 + jnp.exp(-gt)) * up).T.astype(BF16)

    def down_part(i):
        y = jnp.dot(hid[...], wd[:, chunk_of(turn_of(i, z))], preferred_element_type=F32)
        sib_send[i] = y[slots:].reshape(plane, line, cap, wide_n).astype(BF16)
        sib_copy(i).start()
        y_own[i] = y[:slots]

    def finish(i):
        sib_copy(i).wait_recv()
        ret_send[i] = (y_own[i].reshape(plane, line, cap, wide_n) + sib_recv[i].astype(F32)).astype(BF16)
        ret_recv[i, pl.ds(g, 1)] = ret_send[i, pl.ds(g, 1)]
        plane_peers(lambda d: ret_copy(i, d, g).start())

    for i in range(line):
        down_part(i)
        if i > 0:
            finish(i - 1)
    finish(line - 1)

    line_near(lambda s: lr2_copy(z, s).wait_recv())
    local[3].wait()
    aup_copy.wait_recv()
    low = jnp.sum(lr2_recv[...], axis=0).astype(BF16).astype(F32)
    ranks = jnp.broadcast_to(low.reshape(group // per, 1, LANES), (group // per, per, LANES)).reshape(group, LANES)
    ranks = jnp.where(turn, ranks, 0.0).astype(BF16)
    ranks = jnp.where(keep, jnp.dot(ranks, fold, preferred_element_type=F32), 0.0)

    def up_step(i, acc):
        at = pl.multiple_of(i * span, span)
        wide = jnp.concatenate([jnp.where(id_hi == i * sub + s, ranks, 0.0).astype(BF16) for s in range(sub)], axis=1)
        return acc + dot_nt(wide, aup[:, pl.ds(at, span)])

    corr = lax.fori_loop(0, bank // span, up_step, jnp.zeros((group, LANES), F32))
    cor_send[...] = corr.astype(BF16).reshape(plane, line, rows, LANES)
    cor_recv[pl.ds(g, 1)] = cor_send[pl.ds(g, 1)]
    plane_peers(lambda d: cor_copy(d, g).start())

    share = LANES // (2 * feats)

    def mix(i):
        plane_peers(lambda p: ret_copy(i, g, p).wait_recv())
        j = turn_of(i, z)
        if i == line - 1:
            plane_peers(lambda p: cor_copy(g, p).wait_recv())
        for s in range(line):
            back = ret_recv[i, :, s].astype(F32).reshape(block, wide_n).astype(BF16)
            both = line_comb[s]
            routed = jnp.dot(both[:, :block], back, preferred_element_type=F32)
            routed = routed + jnp.dot(both[:, half_l : half_l + block], back, preferred_element_type=F32)
            if i == line - 1:
                delta = []
                for b in range(wide_n // LANES):
                    one = cor_recv[b * share, s].astype(F32)
                    for t in range(1, share):
                        one = one + cor_recv[b * share + t, s].astype(F32)
                    delta.append(one)
                routed = routed + jnp.concatenate(delta, axis=1)
            part_send[i, s] = routed.astype(BF16)
        own_part[pl.ds(j, 1)] = part_send[i, pl.ds(z, 1)].astype(F32)
        line_far(lambda d: part_copy(i, d, z, j).start())

    for i in range(line):
        mix(i)

    for i in range(line):
        line_near(lambda s: part_copy(i, z, s, turn_of(i, s)).wait_recv())
    for j in range(line):
        def add(s, acc):
            return acc + part_recv[far(s), j].astype(F32)

        out_ref[:, j * wide_n : (j + 1) * wide_n] = lax.fori_loop(0, line - 1, add, own_part[j]).astype(BF16)

    adn_copy.wait_send()
    aup_copy.wait_send()
    for i in range(line):
        sib_copy(i).wait_send()

    def drain_line(d):
        comb_copy(d, z).wait_send()
        lr2_copy(d, z).wait_send()
        for i in range(line):
            x_copy(d, z, i).wait_send()
            part_copy(i, d, z, i).wait_send()

    def drain_plane(d):
        lr1_copy(d, g).wait_send()
        cor_copy(d, g).wait_send()
        loop(line, lambda s: col_copy(d, g, s).wait_send())
        loop(line, lambda s: disp_copy(d, g, s).wait_send())
        for i in range(line):
            ret_copy(i, d, g).wait_send()

    line_far(drain_line)
    plane_peers(drain_plane)
    loop(plane, lambda p: loop(line, lambda s: fwd_copy(p, s).wait_send()))


def per_device(tokens, idx, gates, aid, wg, wu, wd, adn, aup):
    devices = lax.axis_size("exp")
    chips = devices // 2
    plane = 1
    while plane * plane < chips:
        plane *= 2
    line = chips // plane
    rows, width = tokens.shape
    top = idx.shape[1]
    half = wd.shape[1]
    feats, bank = adn.shape
    need = 2 * (rows * top // devices + 1)
    cap = -(-need // 8) * 8
    slots = chips * cap
    short = chips * rows * RANK // LANES
    wide_n = width // line
    blocks = lambda *s: pltpu.VMEM(s, BF16)
    full = lambda *s: pltpu.VMEM(s, F32)
    sems = lambda n: pltpu.SemaphoreType.DMA((n,))
    vm = pl.BlockSpec(memory_space=pltpu.VMEM)
    hbm = pl.BlockSpec(memory_space=pl.ANY)
    return pl.pallas_call(
        functools.partial(kernel, line, plane, cap, top),
        out_shape=jax.ShapeDtypeStruct((rows, width), BF16),
        in_specs=[vm, vm, vm, vm, hbm, hbm, hbm, hbm, hbm],
        out_specs=vm,
        scratch_shapes=[
            blocks(half, width), blocks(half, width), blocks(half, width),
            blocks(LANES, bank), blocks(LANES, bank),
            blocks(line, rows, width), blocks(line, rows, LANES), blocks(line, rows, LANES),
            blocks(plane, line, rows, LANES),
            blocks(plane, line, cap, width), blocks(plane, line, cap, width), blocks(plane, line, cap, width),
            blocks(2 * slots, width), blocks(2 * slots, half), full(line, slots, wide_n),
            blocks(line, plane, line, cap, wide_n), blocks(line, plane, line, cap, wide_n),
            full(short, LANES), full(plane, short, LANES), full(short, LANES), full(line, short, LANES),
            blocks(plane, line, rows, LANES), blocks(plane, line, rows, LANES),
            blocks(line, plane, line, cap, wide_n), blocks(line, plane, line, cap, wide_n),
            blocks(line, line, rows, wide_n), blocks(line, line, rows, wide_n), full(line, rows, wide_n),
            sems(3), sems(2), sems(2), sems(2),
            sems(line * line), sems(line * line), sems(line), sems(line),
            sems(plane * line), sems(plane * line), sems(plane * line), sems(plane * line),
            sems(plane * line), sems(plane * line),
            sems(plane), sems(plane), sems(line), sems(line), sems(plane), sems(plane),
            sems(line * plane), sems(line * plane), sems(line * line), sems(line * line), sems(line), sems(line),
        ],
        compiler_params=pltpu.CompilerParams(
            collective_id=0, has_side_effects=True, vmem_limit_bytes=60 * 1024 * 1024
        ),
    )(tokens, idx.T, gates.T, aid.reshape(1, -1), wg.swapaxes(1, 2), wu.swapaxes(1, 2), wd, adn, aup)


def solution(mesh):
    placed = (
        P(("grp", "exp"), None),
        P(("grp", "exp"), None),
        P(("grp", "exp"), None),
        P("grp"),
        P("exp", None, None),
        P("exp", None, None),
        P("exp", None, None),
        P("exp", None),
        P("exp", None),
    )
    return jax.shard_map(
        per_device, mesh=mesh, in_specs=placed, out_specs=P(("grp", "exp"), None), check_vma=False
    )
```

time: 49.1 us -> 44.7 us (0.910)
  Pallas kernels: 47.4 us -> 43 us
    pallas_call x1, Pallas kernels: 47.4 us -> 43 us  [per_device(): pl.pallas_call(functools.partial(kernel, line, plane, cap, top), out_shap...]
where the time goes in v1:
time: 44.7 us; the launch traced here: 44.5 us
  Pallas kernels  43 us (96%)
  local copies, waits for them, and re-layouts  1.47 us (3%)
    pallas_call x1, Pallas kernels, per_device(): pl.pallas_call(functools.partial(kernel, line, plane, cap, top), out_shap...  43 us
    unnamed x1, local copies, waits for them, and re-layouts  1.47 us

profile of v1, /device:TPU:0, one launch (start us, length us, event | category | flops | bytes accessed | tf_op | source)
XLA Modules:
  0.0 44.5 jit_solution(18375788242551059744)
XLA Ops:
  0.0 43.0 %shard_map.91 = bf16[16,2048]{1,0:T(8,128)(2,1)} custom-call(bf16[16,2048]{1,0:T(8,128)(2,1)} %x_ref.1, s32[6,16]{1,0:T(8,128)} %bitcast.7, f32[6,16]{1,0:T(8,128)} %bitcast.8, s32[1,512]{1,0:T(1,128)} %bitcast.9, bf16[1,704,2048]{2,1,0:T(8,128)(2,1)} %bitcast.5, bf16[1,704,2048]{2,1,0:T(8,128)(2,1)} %bitcast.6, bf16[1,704,2048]{2,1,0:T(8,128)(2,1)} %wd_hbm.1, ...), custom_call_target="tpu_custom_call" | custom-call | tf_op jit(solution)/shard_map/pallas_call | solution.py:406
  43.0 1.5 %copy.11 = bf16[16,2048]{1,0:T(8,128)(2,1)} copy(bf16[16,2048]{1,0:T(8,128)(2,1)} %shard_map.91) | data formatting | bytes 131072

commit v2 on v1

v2 whole, which is shorter than its diff:
```python
import functools

import jax
import jax.numpy as jnp
from jax import lax
from jax.experimental import pallas as pl
from jax.experimental.pallas import tpu as pltpu
from jax.sharding import PartitionSpec as P

RANK = 16
LANES = 128
BF16 = jnp.bfloat16
F32 = jnp.float32
MESH = pl.DeviceIdType.MESH


def dot_nt(a, b):
    return lax.dot_general(a, b, (((1,), (1,)), ((), ())), preferred_element_type=F32)


def kernel(
    line, plane, cap, top, x_hbm, idx_hbm, gate_hbm, aid_hbm, wg_hbm, wu_hbm, wd_hbm, adn_hbm, aup_hbm, out_hbm,
    out_ref,    idx_ref, gate_ref, aid_ref, wg, wu, wd, adn, aup, line_x, comb_send, line_comb, pick_ref, col, disp, recv_a, recv_b, xs, gt_ref, up_ref, hid, y_own, sib_send, sib_recv,
    tag_ref, tag_t, keep_ref, lr_send, lr1_recv, lr2_send, lr2_recv, cor_send, cor_recv, ret_send, ret_recv, part_send, part_recv, own_part,
 in_sem, out_sem, w_sem, adl_sem, ad_s, ad_r, x_s, x_r, cb_s, cb_r, col_s, col_r, disp_s, disp_r, fwd_s, fwd_r, l1_s, l1_r,
    l2_s, l2_r, cor_s, cor_r, ret_s, ret_r, part_s, part_r, sib_s, sib_r,
):
    me = lax.axis_index("exp")
    q = lax.div(me, 2)
    c = lax.rem(me, 2)
    z = lax.div(q, plane)
    g = lax.rem(q, plane)
    sib = me + 1 - 2 * c
    rows, width = x_hbm.shape
    feats = adn_hbm.shape[0]
    bank = adn_hbm.shape[1]
    chips = line * plane
    group = chips * rows
    slots = chips * cap
    block = plane * cap
    wide_n = width // line
    off = pl.multiple_of(lax.rem(me * feats, LANES), feats)
    half_l = LANES // 2

    def remote(src, dst, ss, rs, dev):
        return pltpu.make_async_remote_copy(
            src_ref=src, dst_ref=dst, send_sem=ss, recv_sem=rs, device_id={"exp": dev}, device_id_type=MESH
        )

    def dev_z(to):
        return 2 * (to * plane + g) + c

    def dev_g(to):
        return 2 * (z * plane + to) + c

    side = lax.div(2 * z, line)
    mirror = side * z + (1 - side) * (line - 1 - z)

    def far(s):
        d = s + lax.div(s - mirror + line, line)
        return side * d + (1 - side) * (line - 1 - d)

    def loop(n, fn):
        def step(r, carry):
            fn(r)
            return carry

        lax.fori_loop(0, n, step, 0)

    def line_far(fn):
        loop(line - 1, lambda s: fn(far(s)))

    def line_near(fn):
        loop(line - 1, lambda s: fn(far(line - 2 - s)))

    def plane_peers(fn):
        loop(plane - 1, lambda r: fn(lax.rem(g + 1 + r, plane)))

    barrier = pltpu.get_barrier_semaphore()
    if 2 * feats < LANES:
        adn[...] = jnp.zeros_like(adn)
        aup[...] = jnp.zeros_like(aup)

    def greet(dev):
        pl.semaphore_signal(barrier, inc=1, device_id={"exp": dev}, device_id_type=MESH)

    line_far(lambda d: greet(dev_z(d)))
    plane_peers(lambda d: greet(dev_g(d)))
    greet(sib)

    own_rows = pl.ds(off, feats)
    inputs = [
        pltpu.make_async_copy(idx_hbm, idx_ref, in_sem.at[0]),
        pltpu.make_async_copy(gate_hbm, gate_ref, in_sem.at[1]),
        pltpu.make_async_copy(x_hbm, line_x.at[z], in_sem.at[2]),
        pltpu.make_async_copy(aid_hbm, aid_ref, in_sem.at[3]),
    ]
    for cp in inputs:
        cp.start()
    local = [
        pltpu.make_async_copy(adn_hbm, adn.at[own_rows], adl_sem.at[0]),
        pltpu.make_async_copy(wg_hbm.at[0], wg, w_sem.at[0]),
        pltpu.make_async_copy(wu_hbm.at[0], wu, w_sem.at[1]),
        pltpu.make_async_copy(aup_hbm, aup.at[own_rows], adl_sem.at[1]),
        pltpu.make_async_copy(wd_hbm.at[0], wd, w_sem.at[2]),
    ]
    for cp in inputs:
        cp.wait()
    for cp in local:
        cp.start()
    pl.semaphore_wait(barrier, line + plane - 1)

    def step_of(k, at):
        return at if k == 0 else k - 1 + lax.div(k - 1 + line - at, line)

    def lanes_of(chip):
        return pl.ds(pl.multiple_of(lax.div(chip * 2 * feats, LANES) * LANES, LANES), LANES)

    def chunk_of(i):
        return pl.ds(pl.multiple_of(i * wide_n, wide_n), wide_n)

    def x_copy(to, slot, i, kind):
        at = chunk_of(i)
        return remote(line_x.at[z, :, at], line_x.at[slot, :, at], x_s.at[0], x_r.at[kind * line + slot], dev_z(to))

    def comb_copy(to, slot):
        return remote(comb_send.at[to], line_comb.at[slot], cb_s.at[0], cb_r.at[slot], dev_z(to))

    def col_copy(to, slot, s):
        return remote(
            line_x.at[s, :, lanes_of(z * plane + to)], col.at[slot, s], col_s.at[0], col_r.at[0], dev_g(to)
        )

    def disp_copy(to, slot, s, k):
        at = chunk_of(step_of(k, z))
        return remote(disp.at[to, s, :, at], recv_a.at[slot, s, :, at], disp_s.at[0], disp_r.at[k], dev_g(to))

    def fwd_copy(k):
        at = chunk_of(step_of(k, z))
        return remote(recv_a.at[:, :, :, at], recv_b.at[:, :, :, at], fwd_s.at[k], fwd_r.at[k], sib)

    def lr1_copy(to, slot):
        return remote(lr_send, lr1_recv.at[slot], l1_s.at[0], l1_r.at[0], dev_g(to))

    def lr2_copy(to, slot):
        return remote(lr2_send, lr2_recv.at[slot], l2_s.at[0], l2_r.at[0], dev_z(to))

    def cor_copy(to, slot):
        return remote(cor_send.at[to], cor_recv.at[slot], cor_s.at[0], cor_r.at[0], dev_g(to))

    def ret_copy(i, to, slot):
        return remote(ret_send.at[i, to], ret_recv.at[i, slot], ret_s.at[0], ret_r.at[i], dev_g(to))

    def turn_of(i, at):
        return lax.rem(at + 1 + i, line)

    def part_copy(i, to, slot, j):
        return remote(part_send.at[i, to], part_recv.at[slot, j], part_s.at[0], part_r.at[0], dev_z(to))

    def sib_copy(i):
        return remote(sib_send.at[i], sib_recv.at[i], sib_s.at[i], sib_r.at[i], sib)

    rest_z = pl.ds(0, line - 1)
    rest_g = pl.ds(0, plane - 1)
    all_x = remote(line_x.at[rest_z], line_x.at[rest_z], x_s.at[0], x_r.at[0], sib)
    all_comb = remote(comb_send.at[rest_z], line_comb.at[rest_z], cb_s.at[0], cb_r.at[0], sib)
    all_col = remote(col.at[rest_g], col.at[rest_g], col_s.at[0], col_r.at[0], sib)
    all_disp = remote(disp.at[rest_g], recv_a.at[rest_g], disp_s.at[0], disp_r.at[0], sib)
    all_lr1 = remote(lr1_recv.at[rest_g], lr1_recv.at[rest_g], l1_s.at[0], l1_r.at[0], sib)
    all_lr2 = remote(lr2_recv.at[rest_z], lr2_recv.at[rest_z], l2_s.at[0], l2_r.at[0], sib)
    all_cor = remote(cor_send.at[rest_g], cor_recv.at[rest_g], cor_s.at[0], cor_r.at[0], sib)
    all_ret = remote(ret_send.at[:, rest_g], ret_recv.at[:, rest_g], ret_s.at[0], ret_r.at[0], sib)
    all_part = remote(part_send.at[:, rest_z], part_recv.at[rest_z], part_s.at[0], part_r.at[0], sib)

    def some_x(s, k):
        at = chunk_of(0)
        return remote(line_x.at[s, :, at], line_x.at[s, :, at], x_s.at[0], x_r.at[k * line + s], sib)

    def some_disp(k):
        at = chunk_of(0)
        return remote(disp.at[rest_g, :, :, at], recv_a.at[rest_g, :, :, at], disp_s.at[0], disp_r.at[k], sib)

    def some_ret(i):
        return remote(ret_send.at[i, rest_g], ret_recv.at[i, rest_g], ret_s.at[0], ret_r.at[i], sib)

    line_far(lambda d: x_copy(d, z, step_of(0, d), 0).start())
    plane_peers(lambda d: col_copy(d, g, z).start())
    slot = lax.broadcasted_iota(jnp.int32, (slots, rows), 0)
    slot_e = lax.div(slot, cap)
    chosen = jnp.zeros((slots, rows), F32)
    weight = jnp.zeros((slots, rows), F32)
    for k in range(top):
        hit = idx_ref[k : k + 1, :] == slot_e
        chosen = chosen + jnp.where(hit, 1.0, 0.0)
        weight = weight + jnp.where(hit, gate_ref[k : k + 1, :], 0.0)
    earlier = jnp.where(
        lax.broadcasted_iota(jnp.int32, (rows, rows), 0) < lax.broadcasted_iota(jnp.int32, (rows, rows), 1), 1.0, 0.0
    )
    rank_of = jnp.dot(chosen.astype(BF16), earlier.astype(BF16), preferred_element_type=F32)
    slot_p = lax.rem(slot, cap).astype(F32)
    combine = jnp.where((chosen > 0.5) & (rank_of == slot_p), weight, 0.0)
    for d in range(line):
        part = combine[d * block : (d + 1) * block].T
        hi = part.astype(BF16)
        lo = (part - hi.astype(F32)).astype(BF16)
        comb_send[d, :, :block] = hi
        comb_send[d, :, half_l : half_l + block] = lo
    line_comb[pl.ds(z, 1)] = comb_send[pl.ds(z, 1)]

    line_far(lambda d: comb_copy(d, z).start())
    for k in range(1, line):
        line_far(lambda d: x_copy(d, z, step_of(k, d), k).start())
    adn_copy = remote(adn_hbm, adn.at[own_rows], ad_s.at[0], ad_r.at[0], sib)
    aup_copy = remote(aup_hbm, aup.at[own_rows], ad_s.at[1], ad_r.at[1], sib)
    adn_copy.start()
    aup_copy.start()

    def own_col(s):
        col[pl.ds(g, 1), pl.ds(s, 1)] = line_x[pl.ds(s, 1), :, lanes_of(q)].reshape(1, 1, rows, LANES)

    def take_pick(s):
        pick = jnp.where(line_comb[s].astype(F32) > 0.0, 1.0, 0.0).T[:block]
        pick_ref[pl.ds(s, 1)] = pick.astype(BF16).reshape(1, block, rows)

    def pack(s, k):
        at = chunk_of(step_of(k, z))
        packed = jnp.dot(pick_ref[s], line_x[s, :, at], preferred_element_type=F32)
        disp[:, pl.ds(s, 1), :, at] = packed.reshape(plane, 1, cap, wide_n).astype(BF16)
        recv_a[pl.ds(g, 1), pl.ds(s, 1), :, at] = disp[pl.ds(g, 1), pl.ds(s, 1), :, at]
        plane_peers(lambda d: disp_copy(d, g, s, k).start())

    take_pick(z)
    for k in range(line):
        pack(z, k)
    own_col(z)

    near_z = [far(line - 2 - k) for k in range(line - 1)]
    half = wd.shape[0]
    cut = -(-half // (2 * LANES)) * LANES

    def relay(k):
        for s in near_z:
            some_x(s, k).wait_recv()
            if k == 0:
                plane_peers(lambda d: col_copy(d, g, s).start())
                own_col(s)
                comb_copy(z, s).wait_recv()
                take_pick(s)
            pack(s, k)

    def receive(k):
        at = chunk_of(step_of(k, z))
        some_disp(k).wait_recv()
        fwd_copy(k).start()
        xs[:slots, at] = recv_a[:, :, :, at].astype(F32).reshape(slots, wide_n).astype(BF16)

    def multiply(k):
        at = chunk_of(step_of(k, z))
        fwd_copy(k).wait_recv()
        xs[slots:, at] = recv_b[:, :, :, at].astype(F32).reshape(slots, wide_n).astype(BF16)
        if k == 0:
            local[1].wait()
            local[2].wait()
        for a, b in ((0, cut), (cut, half)):
            gt = dot_nt(wg[a:b, at], xs[:, at])
            up = dot_nt(wu[a:b, at], xs[:, at])
            if k > 0:
                gt = gt + gt_ref[a:b]
                up = up + up_ref[a:b]
            if k < line - 1:
                gt_ref[a:b] = gt
                up_ref[a:b] = up
            else:
                hid[:, a:b] = (gt / (1.0 + jnp.exp(-gt)) * up).T.astype(BF16)

    relay(0)
    per = LANES // RANK
    ids = []
    near = line * rows
    for p in range(plane):
        lane = lax.broadcasted_iota(jnp.int32, (near, aid_ref.shape[1]), 1)
        row = lax.broadcasted_iota(jnp.int32, (near, aid_ref.shape[1]), 0)
        here = ((lax.div(row, rows) * plane + p) * 2 + c) * rows + lax.rem(row, rows)
        ids.append(jnp.sum(jnp.where(lane == here, aid_ref[...].astype(F32), 0.0), axis=1, keepdims=True))
    ids = jnp.broadcast_to(jnp.concatenate(ids, axis=0), (group, LANES)).astype(jnp.int32)
    id_hi = lax.div(ids, per)
    id_lo = ids - id_hi * per
    tag_ref[...] = id_hi.astype(F32).astype(BF16)
    tag_t[...] = id_hi.astype(F32).T.astype(BF16)
    lane_g = lax.broadcasted_iota(jnp.int32, (group, LANES), 1)
    keep_ref[...] = jnp.where(lax.div(lane_g, RANK) == id_lo, 1.0, 0.0)

    for k in range(1, line):
        relay(k)
    for k in range(line // 2):
        receive(k)
    all_col.wait_recv()
    local[0].wait()
    adn_copy.wait_recv()
    cols = col[...].reshape(group, LANES)
    blocks = bank // LANES

    def masked(v, t, k):
        return jnp.where(t == jnp.asarray(k, BF16), v, jnp.zeros_like(v))

    tag = tag_ref[...]

    terms = jnp.zeros((group, LANES), F32)
    for k in range(0, blocks, 2):
        wide = jnp.concatenate([masked(cols, tag, k), masked(cols, tag, k + 1)], axis=1)
        tall = jnp.concatenate([adn[:, k * LANES : (k + 1) * LANES], adn[:, (k + 1) * LANES : (k + 2) * LANES]], axis=0)
        terms = terms + jnp.dot(wide, tall, preferred_element_type=F32)
    terms = (terms * keep_ref[...]).astype(BF16)
    fi = lax.broadcasted_iota(jnp.int32, (LANES, LANES), 0)
    fj = lax.broadcasted_iota(jnp.int32, (LANES, LANES), 1)
    fold = jnp.where(lax.rem(fi, RANK) == lax.rem(fj, RANK), 1.0, 0.0).astype(BF16)
    turn = lax.div(lane_g, RANK) == lax.rem(lax.broadcasted_iota(jnp.int32, (group, LANES), 0), per)
    folded = jnp.where(turn, jnp.dot(terms, fold, preferred_element_type=F32), 0.0)
    lr_send[...] = jnp.sum(folded.reshape(group // per, per, LANES), axis=1)
    lr1_recv[pl.ds(g, 1)] = lr_send[...].reshape(1, group // per, LANES)
    plane_peers(lambda d: lr1_copy(d, g).start())

    for k in range(line // 2, line):
        receive(k)
    for k in range(line - 1):
        multiply(k)
    multiply(line - 1)
    local[4].wait()

    def down_part(i):
        y = jnp.dot(hid[...], wd[:, chunk_of(turn_of(i, z))], preferred_element_type=F32)
        sib_send[i] = y[slots:].reshape(plane, line, cap, wide_n).astype(BF16)
        sib_copy(i).start()
        y_own[i] = y[:slots]

    def finish(i):
        sib_copy(i).wait_recv()
        ret_send[i] = (y_own[i].reshape(plane, line, cap, wide_n) + sib_recv[i].astype(F32)).astype(BF16)
        ret_recv[i, pl.ds(g, 1)] = ret_send[i, pl.ds(g, 1)]
        plane_peers(lambda d: ret_copy(i, d, g).start())

    for i in range(line):
        down_part(i)
    all_lr1.wait_recv()
    lr2_send[...] = jnp.sum(lr1_recv[...], axis=0)
    lr2_recv[pl.ds(z, 1)] = lr2_send[...].reshape(1, group // per, LANES)
    line_far(lambda d: lr2_copy(d, z).start())
    for i in range(line):
        finish(i)

    all_lr2.wait_recv()
    local[3].wait()
    aup_copy.wait_recv()
    low = jnp.sum(lr2_recv[...], axis=0).astype(BF16).astype(F32)
    ranks = jnp.broadcast_to(low.reshape(group // per, 1, LANES), (group // per, per, LANES)).reshape(group, LANES)
    ranks = jnp.where(turn, ranks, 0.0).astype(BF16)
    ranks = jnp.dot(ranks, fold, preferred_element_type=F32) * keep_ref[...]
    ranks = ranks.T.astype(BF16)
    tag = tag_t[...]
    corr = jnp.zeros((LANES, group), F32)
    for k in range(0, blocks, 2):
        tall = jnp.concatenate([masked(ranks, tag, k), masked(ranks, tag, k + 1)], axis=0)
        corr = corr + jnp.dot(aup[:, k * LANES : (k + 2) * LANES], tall, preferred_element_type=F32)
    cor_send[...] = corr.T.astype(BF16).reshape(plane, line, rows, LANES)
    cor_recv[pl.ds(g, 1)] = cor_send[pl.ds(g, 1)]
    plane_peers(lambda d: cor_copy(d, g).start())

    share = LANES // (2 * feats)

    def mix(i):
        some_ret(i).wait_recv()
        j = turn_of(i, z)
        if i == line - 1:
            all_cor.wait_recv()
        for s in range(line):
            back = ret_recv[i, :, s].astype(F32).reshape(block, wide_n).astype(BF16)
            both = line_comb[s]
            routed = jnp.dot(both[:, :block], back, preferred_element_type=F32)
            routed = routed + jnp.dot(both[:, half_l : half_l + block], back, preferred_element_type=F32)
            if i == line - 1:
                delta = []
                for b in range(wide_n // LANES):
                    one = cor_recv[b * share, s].astype(F32)
                    for t in range(1, share):
                        one = one + cor_recv[b * share + t, s].astype(F32)
                    delta.append(one)
                routed = routed + jnp.concatenate(delta, axis=1)
            part_send[i, s] = routed.astype(BF16)
        own_part[pl.ds(j, 1)] = part_send[i, pl.ds(z, 1)].astype(F32)
        line_far(lambda d: part_copy(i, d, z, j).start())

    for i in range(line):
        mix(i)

    for cp in (all_x, all_comb, all_col, all_disp, all_lr1, all_lr2, all_cor, all_ret):
        cp.wait_send()
    adn_copy.wait_send()
    aup_copy.wait_send()
    for i in range(line):
        sib_copy(i).wait_send()
        fwd_copy(i).wait_send()
    all_part.wait_recv()
    for j in range(line):
        def add(s, acc):
            return acc + part_recv[far(s), j].astype(F32)

        out_ref[:, j * wide_n : (j + 1) * wide_n] = lax.fori_loop(0, line - 1, add, own_part[j]).astype(BF16)

    out_copy = pltpu.make_async_copy(out_ref, out_hbm, out_sem.at[0])
    out_copy.start()
    all_part.wait_send()
    out_copy.wait()


def per_device(tokens, idx, gates, aid, wg, wu, wd, adn, aup):
    devices = lax.axis_size("exp")
    chips = devices // 2
    plane = 1
    while plane * plane < chips:
        plane *= 2
    line = chips // plane
    rows, width = tokens.shape
    top = idx.shape[1]
    half = wd.shape[1]
    feats, bank = adn.shape
    need = 2 * (rows * top // devices + 1)
    cap = -(-need // 8) * 8
    slots = chips * cap
    group = chips * rows
    short = chips * rows * RANK // LANES
    wide_n = width // line
    blocks = lambda *s: pltpu.VMEM(s, BF16)
    full = lambda *s: pltpu.VMEM(s, F32)
    sems = lambda n: pltpu.SemaphoreType.DMA((n,))
    hbm = pl.BlockSpec(memory_space=pl.ANY)
    return pl.pallas_call(
        functools.partial(kernel, line, plane, cap, top),
        out_shape=jax.ShapeDtypeStruct((rows, width), BF16),
        in_specs=[hbm] * 9,
        out_specs=hbm,
        scratch_shapes=[
            blocks(rows, width), pltpu.VMEM((top, rows), jnp.int32), full(top, rows), pltpu.VMEM((1, aid.shape[0]), jnp.int32),
            blocks(half, width), blocks(half, width), blocks(half, width),
            blocks(LANES, bank), blocks(LANES, bank),
            blocks(line, rows, width), blocks(line, rows, LANES), blocks(line, rows, LANES),
            blocks(line, plane * cap, rows),
            blocks(plane, line, rows, LANES),
            blocks(plane, line, cap, width), blocks(plane, line, cap, width), blocks(plane, line, cap, width),
            blocks(2 * slots, width), full(half, 2 * slots), full(half, 2 * slots), blocks(2 * slots, half),
            full(line, slots, wide_n),
            blocks(line, plane, line, cap, wide_n), blocks(line, plane, line, cap, wide_n),
            blocks(group, LANES), blocks(LANES, group), full(group, LANES),
            full(short, LANES), full(plane, short, LANES), full(short, LANES), full(line, short, LANES),
            blocks(plane, line, rows, LANES), blocks(plane, line, rows, LANES),
            blocks(line, plane, line, cap, wide_n), blocks(line, plane, line, cap, wide_n),
            blocks(line, line, rows, wide_n), blocks(line, line, rows, wide_n), full(line, rows, wide_n),
            sems(4), sems(1), sems(3), sems(2), sems(2), sems(2),
            sems(1), sems(line * line), sems(1), sems(line), sems(1), sems(1), sems(1), sems(line), sems(line), sems(line),
            sems(1), sems(1), sems(1), sems(1), sems(1), sems(1), sems(1), sems(line), sems(1), sems(1),
            sems(line), sems(line),
        ],
        compiler_params=pltpu.CompilerParams(
            collective_id=0, has_side_effects=True, vmem_limit_bytes=60 * 1024 * 1024
        ),
    )(tokens, idx.T, gates.T, aid.reshape(1, -1), wg.swapaxes(1, 2), wu.swapaxes(1, 2), wd, adn, aup)


def solution(mesh):
    placed = (
        P(("grp", "exp"), None),
        P(("grp", "exp"), None),
        P(("grp", "exp"), None),
        P("grp"),
        P("exp", None, None),
        P("exp", None, None),
        P("exp", None, None),
        P("exp", None),
        P("exp", None),
    )
    return jax.shard_map(
        per_device, mesh=mesh, in_specs=placed, out_specs=P(("grp", "exp"), None), check_vma=False
    )
```

time: 44.7 us -> 36.7 us (0.82)
  Pallas kernels: 43 us -> 35 us
    pallas_call x1, Pallas kernels: 43 us -> 35 us  [per_device(): pl.pallas_call(functools.partial(kernel, line, plane, cap, top), out_shap...]
where the time goes in v2:
time: 36.7 us; the launch traced here: 36.5 us
  Pallas kernels  35 us (95%)
  local copies, waits for them, and re-layouts  1.47 us (4%)
    pallas_call x1, Pallas kernels, per_device(): pl.pallas_call(functools.partial(kernel, line, plane, cap, top), out_shap...  35 us
    unnamed x1, local copies, waits for them, and re-layouts  1.47 us

profile of v2, /device:TPU:0, one launch (start us, length us, event | category | flops | bytes accessed | tf_op | source)
XLA Modules:
  0.0 36.5 jit_solution(9042356951405588906)
XLA Ops:
  0.0 35.0 %shard_map.91 = bf16[16,2048]{1,0:T(8,128)(2,1)} custom-call(bf16[16,2048]{1,0:T(8,128)(2,1)} %x_hbm.1, s32[6,16]{1,0:T(8,128)} %bitcast.7, f32[6,16]{1,0:T(8,128)} %bitcast.8, s32[1,512]{1,0:T(1,128)} %bitcast.9, bf16[1,704,2048]{2,1,0:T(8,128)(2,1)} %bitcast.5, bf16[1,704,2048]{2,1,0:T(8,128)(2,1)} %bitcast.6, bf16[1,704,2048]{2,1,0:T(8,128)(2,1)} %wd_hbm.1, ...), custom_call_target="tpu_custom_call" | custom-call | tf_op jit(solution)/shard_map/pallas_call | solution.py:436
  35.0 1.5 %copy.11 = bf16[16,2048]{1,0:T(8,128)(2,1)} copy(bf16[16,2048]{1,0:T(8,128)(2,1)} %shard_map.91) | data formatting | bytes 131072

commit v3 on v2

--- a/solution.py
+++ b/solution.py
@@ -19,11 +19,12 @@
 
 
 def kernel(
-    line, plane, cap, top, x_hbm, idx_hbm, gate_hbm, aid_hbm, wg_hbm, wu_hbm, wd_hbm, adn_hbm, aup_hbm, out_hbm,
-    out_ref,    idx_ref, gate_ref, aid_ref, wg, wu, wd, adn, aup, line_x, comb_send, line_comb, pick_ref, col, disp, recv_a, recv_b, xs, gt_ref, up_ref, hid, y_own, sib_send, sib_recv,
-    tag_ref, tag_t, keep_ref, lr_send, lr1_recv, lr2_send, lr2_recv, cor_send, cor_recv, ret_send, ret_recv, part_send, part_recv, own_part,
- in_sem, out_sem, w_sem, adl_sem, ad_s, ad_r, x_s, x_r, cb_s, cb_r, col_s, col_r, disp_s, disp_r, fwd_s, fwd_r, l1_s, l1_r,
-    l2_s, l2_r, cor_s, cor_r, ret_s, ret_r, part_s, part_r, sib_s, sib_r,
+    line, plane, cap, top, x_hbm, idx_hbm, gate_hbm, aid_hbm, wg_hbm, wu_hbm, wd_hbm, adn_hbm, aup_hbm, out_ref,
+    idx_ref, gate_ref, aid_ref, wg, wu, wd, adn, aup, line_x, comb_send, line_comb, pick_ref, col, disp, recv_a,
+    recv_b, xs, gt_ref, up_ref, hid, sib_send, sib_recv, tag_ref, tag_t, keep_ref, lr_send, lr1_recv, lr2_send,
+    lr2_recv, cor_send, cor_recv, ret_send, ret_recv, part_send, part_recv, own_part, in_sem, w_sem, adl_sem, ad_s,
+    ad_r, x_s, x_r, cb_s, cb_r, col_s, col_r, disp_s, disp_r, fwd_s, fwd_r, l1_s, l1_r, l2_s, l2_r, cor_s, cor_r,
+    ret_s, ret_r, part_s, part_r, sib_s, sib_r,
 ):
     me = lax.axis_index("exp")
     q = lax.div(me, 2)
@@ -53,6 +54,9 @@
     def dev_g(to):
         return 2 * (z * plane + to) + c
 
+    def dev_cross(to):
+        return 2 * (z * plane + to) + 1 - c
+
     side = lax.div(2 * z, line)
     mirror = side * z + (1 - side) * (line - 1 - z)
 
@@ -86,6 +90,7 @@
 
     line_far(lambda d: greet(dev_z(d)))
     plane_peers(lambda d: greet(dev_g(d)))
+    plane_peers(lambda d: greet(dev_cross(d)))
     greet(sib)
 
     own_rows = pl.ds(off, feats)
@@ -108,7 +113,7 @@
         cp.wait()
     for cp in local:
         cp.start()
-    pl.semaphore_wait(barrier, line + plane - 1)
+    pl.semaphore_wait(barrier, line + 2 * plane - 2)
 
     def step_of(k, at):
         return at if k == 0 else k - 1 + lax.div(k - 1 + line - at, line)
@@ -126,9 +131,10 @@
     def comb_copy(to, slot):
         return remote(comb_send.at[to], line_comb.at[slot], cb_s.at[0], cb_r.at[slot], dev_z(to))
 
-    def col_copy(to, slot, s):
+    def col_copy(to, s):
         return remote(
-            line_x.at[s, :, lanes_of(z * plane + to)], col.at[slot, s], col_s.at[0], col_r.at[0], dev_g(to)
+            line_x.at[s, :, lanes_of(z * plane + to)], col.at[c, g, s],
+            col_s.at[0], col_r.at[c], 2 * (z * plane + to) + 1,
         )
 
     def disp_copy(to, slot, s, k):
@@ -139,8 +145,10 @@
         at = chunk_of(step_of(k, z))
         return remote(recv_a.at[:, :, :, at], recv_b.at[:, :, :, at], fwd_s.at[k], fwd_r.at[k], sib)
 
-    def lr1_copy(to, slot):
-        return remote(lr_send, lr1_recv.at[slot], l1_s.at[0], l1_r.at[0], dev_g(to))
+    def lr1_copy(par, to):
+        return remote(
+            lr_send.at[par], lr1_recv.at[g], l1_s.at[par], l1_r.at[0], 2 * (z * plane + to) + par
+        )
 
     def lr2_copy(to, slot):
         return remote(lr2_send, lr2_recv.at[slot], l2_s.at[0], l2_r.at[0], dev_z(to))
@@ -164,9 +172,11 @@
     rest_g = pl.ds(0, plane - 1)
     all_x = remote(line_x.at[rest_z], line_x.at[rest_z], x_s.at[0], x_r.at[0], sib)
     all_comb = remote(comb_send.at[rest_z], line_comb.at[rest_z], cb_s.at[0], cb_r.at[0], sib)
-    all_col = remote(col.at[rest_g], col.at[rest_g], col_s.at[0], col_r.at[0], sib)
+    some_col = remote(col.at[1, rest_g], col.at[1, rest_g], col_s.at[0], col_r.at[1], sib)
+    all_col = remote(col.at[0], col.at[0], col_s.at[0], col_r.at[0], sib)
     all_disp = remote(disp.at[rest_g], recv_a.at[rest_g], disp_s.at[0], disp_r.at[0], sib)
-    all_lr1 = remote(lr1_recv.at[rest_g], lr1_recv.at[rest_g], l1_s.at[0], l1_r.at[0], sib)
+    some_lr1 = remote(lr1_recv.at[rest_g], lr1_recv.at[rest_g], l1_s.at[1], l1_r.at[0], sib)
+    all_lr1 = remote(lr1_recv, lr1_recv, l1_s.at[0], l1_r.at[0], sib)
     all_lr2 = remote(lr2_recv.at[rest_z], lr2_recv.at[rest_z], l2_s.at[0], l2_r.at[0], sib)
     all_cor = remote(cor_send.at[rest_g], cor_recv.at[rest_g], cor_s.at[0], cor_r.at[0], sib)
     all_ret = remote(ret_send.at[:, rest_g], ret_recv.at[:, rest_g], ret_s.at[0], ret_r.at[0], sib)
@@ -184,7 +194,7 @@
         return remote(ret_send.at[i, rest_g], ret_recv.at[i, rest_g], ret_s.at[0], ret_r.at[i], sib)
 
     line_far(lambda d: x_copy(d, z, step_of(0, d), 0).start())
-    plane_peers(lambda d: col_copy(d, g, z).start())
+    plane_peers(lambda d: col_copy(d, z).start())
     slot = lax.broadcasted_iota(jnp.int32, (slots, rows), 0)
     slot_e = lax.div(slot, cap)
     chosen = jnp.zeros((slots, rows), F32)
@@ -216,7 +226,13 @@
     aup_copy.start()
 
     def own_col(s):
-        col[pl.ds(g, 1), pl.ds(s, 1)] = line_x[pl.ds(s, 1), :, lanes_of(q)].reshape(1, 1, rows, LANES)
+        @pl.when(c == 1)
+        def _():
+            col[1, pl.ds(g, 1), pl.ds(s, 1)] = line_x[pl.ds(s, 1), :, lanes_of(q)].reshape(1, 1, rows, LANES)
+
+        @pl.when(c == 0)
+        def _():
+            col_copy(g, s).start()
 
     def take_pick(s):
         pick = jnp.where(line_comb[s].astype(F32) > 0.0, 1.0, 0.0).T[:block]
@@ -242,7 +258,7 @@
         for s in near_z:
             some_x(s, k).wait_recv()
             if k == 0:
-                plane_peers(lambda d: col_copy(d, g, s).start())
+                plane_peers(lambda d: col_copy(d, s).start())
                 own_col(s)
                 comb_copy(z, s).wait_recv()
                 take_pick(s)
@@ -273,76 +289,100 @@
             else:
                 hid[:, a:b] = (gt / (1.0 + jnp.exp(-gt)) * up).T.astype(BF16)
 
+    per = LANES // RANK
+    near = line * rows
+    lane_g = lax.broadcasted_iota(jnp.int32, (group, LANES), 1)
+    own = jnp.zeros((group, LANES), jnp.int32)
+    for par in range(2):
+        ids = []
+        for p in range(plane):
+            lane = lax.broadcasted_iota(jnp.int32, (near, aid_ref.shape[1]), 1)
+            row = lax.broadcasted_iota(jnp.int32, (near, aid_ref.shape[1]), 0)
+            here = ((lax.div(row, rows) * plane + p) * 2 + par) * rows + lax.rem(row, rows)
+            ids.append(jnp.sum(jnp.where(lane == here, aid_ref[...].astype(F32), 0.0), axis=1, keepdims=True))
+        ids = jnp.broadcast_to(jnp.concatenate(ids, axis=0), (group, LANES)).astype(jnp.int32)
+        id_hi = lax.div(ids, per)
+        tag_ref[par] = id_hi.astype(F32).astype(BF16)
+        keep_ref[par] = jnp.where(lax.div(lane_g, RANK) == ids - id_hi * per, 1.0, 0.0)
+        own = jnp.where(c == par, id_hi, own)
+    tag_t[...] = own.astype(F32).T.astype(BF16)
     relay(0)
-    per = LANES // RANK
-    ids = []
-    near = line * rows
-    for p in range(plane):
-        lane = lax.broadcasted_iota(jnp.int32, (near, aid_ref.shape[1]), 1)
-        row = lax.broadcasted_iota(jnp.int32, (near, aid_ref.shape[1]), 0)
-        here = ((lax.div(row, rows) * plane + p) * 2 + c) * rows + lax.rem(row, rows)
-        ids.append(jnp.sum(jnp.where(lane == here, aid_ref[...].astype(F32), 0.0), axis=1, keepdims=True))
-    ids = jnp.broadcast_to(jnp.concatenate(ids, axis=0), (group, LANES)).astype(jnp.int32)
-    id_hi = lax.div(ids, per)
-    id_lo = ids - id_hi * per
-    tag_ref[...] = id_hi.astype(F32).astype(BF16)
-    tag_t[...] = id_hi.astype(F32).T.astype(BF16)
-    lane_g = lax.broadcasted_iota(jnp.int32, (group, LANES), 1)
-    keep_ref[...] = jnp.where(lax.div(lane_g, RANK) == id_lo, 1.0, 0.0)
-
     for k in range(1, line):
         relay(k)
-    for k in range(line // 2):
-        receive(k)
-    all_col.wait_recv()
-    local[0].wait()
-    adn_copy.wait_recv()
-    cols = col[...].reshape(group, LANES)
     blocks = bank // LANES
 
     def masked(v, t, k):
         return jnp.where(t == jnp.asarray(k, BF16), v, jnp.zeros_like(v))
 
-    tag = tag_ref[...]
-
-    terms = jnp.zeros((group, LANES), F32)
-    for k in range(0, blocks, 2):
-        wide = jnp.concatenate([masked(cols, tag, k), masked(cols, tag, k + 1)], axis=1)
-        tall = jnp.concatenate([adn[:, k * LANES : (k + 1) * LANES], adn[:, (k + 1) * LANES : (k + 2) * LANES]], axis=0)
-        terms = terms + jnp.dot(wide, tall, preferred_element_type=F32)
-    terms = (terms * keep_ref[...]).astype(BF16)
     fi = lax.broadcasted_iota(jnp.int32, (LANES, LANES), 0)
     fj = lax.broadcasted_iota(jnp.int32, (LANES, LANES), 1)
     fold = jnp.where(lax.rem(fi, RANK) == lax.rem(fj, RANK), 1.0, 0.0).astype(BF16)
     turn = lax.div(lane_g, RANK) == lax.rem(lax.broadcasted_iota(jnp.int32, (group, LANES), 0), per)
-    folded = jnp.where(turn, jnp.dot(terms, fold, preferred_element_type=F32), 0.0)
-    lr_send[...] = jnp.sum(folded.reshape(group // per, per, LANES), axis=1)
-    lr1_recv[pl.ds(g, 1)] = lr_send[...].reshape(1, group // per, LANES)
-    plane_peers(lambda d: lr1_copy(d, g).start())
-
+
+    def down(par):
+        cols = col[par].reshape(group, LANES)
+        tag = tag_ref[par]
+        terms = jnp.zeros((group, LANES), F32)
+        for k in range(0, blocks, 2):
+            wide = jnp.concatenate([masked(cols, tag, k), masked(cols, tag, k + 1)], axis=1)
+            tall = jnp.concatenate(
+                [adn[:, k * LANES : (k + 1) * LANES], adn[:, (k + 1) * LANES : (k + 2) * LANES]], axis=0
+            )
+            terms = terms + jnp.dot(wide, tall, preferred_element_type=F32)
+        terms = (terms * keep_ref[par]).astype(BF16)
+        folded = jnp.where(turn, jnp.dot(terms, fold, preferred_element_type=F32), 0.0)
+        lr_send[par] = jnp.sum(folded.reshape(group // per, per, LANES), axis=1).astype(BF16)
+        plane_peers(lambda d: lr1_copy(par, d).start())
+
+    local[0].wait()
+    adn_copy.wait_recv()
+
+    @pl.when(c == 1)
+    def _():
+        some_col.wait_recv()
+        down(1)
+        lr1_recv[pl.ds(g, 1)] = lr_send[1].reshape(1, group // per, LANES)
+
+    for k in range(line // 2):
+        receive(k)
     for k in range(line // 2, line):
         receive(k)
+    @pl.when(c == 1)
+    def _():
+        all_col.wait_recv()
+        down(0)
+        lr1_copy(0, g).start()
+
     for k in range(line - 1):
         multiply(k)
     multiply(line - 1)
     local[4].wait()
 
-    def down_part(i):
-        y = jnp.dot(hid[...], wd[:, chunk_of(turn_of(i, z))], preferred_element_type=F32)
-        sib_send[i] = y[slots:].reshape(plane, line, cap, wide_n).astype(BF16)
+    def down_sib(i):
+        at = chunk_of(turn_of(i, z))
+        y = jnp.dot(hid[slots:], wd[:, at], preferred_element_type=F32)
+        sib_send[i] = y.reshape(plane, line, cap, wide_n).astype(BF16)
         sib_copy(i).start()
-        y_own[i] = y[:slots]
 
     def finish(i):
+        at = chunk_of(turn_of(i, z))
+        y = jnp.dot(hid[:slots], wd[:, at], preferred_element_type=F32).reshape(plane, line, cap, wide_n)
         sib_copy(i).wait_recv()
-        ret_send[i] = (y_own[i].reshape(plane, line, cap, wide_n) + sib_recv[i].astype(F32)).astype(BF16)
+        ret_send[i] = (y + sib_recv[i].astype(F32)).astype(BF16)
         ret_recv[i, pl.ds(g, 1)] = ret_send[i, pl.ds(g, 1)]
         plane_peers(lambda d: ret_copy(i, d, g).start())
 
     for i in range(line):
-        down_part(i)
-    all_lr1.wait_recv()
-    lr2_send[...] = jnp.sum(lr1_recv[...], axis=0)
+        down_sib(i)
+    @pl.when(c == 1)
+    def _():
+        some_lr1.wait_recv()
+
+    @pl.when(c == 0)
+    def _():
+        all_lr1.wait_recv()
+
+    lr2_send[...] = jnp.sum(lr1_recv[...].astype(F32), axis=0).astype(BF16)
     lr2_recv[pl.ds(z, 1)] = lr2_send[...].reshape(1, group // per, LANES)
     line_far(lambda d: lr2_copy(d, z).start())
     for i in range(line):
@@ -351,10 +391,10 @@
     all_lr2.wait_recv()
     local[3].wait()
     aup_copy.wait_recv()
-    low = jnp.sum(lr2_recv[...], axis=0).astype(BF16).astype(F32)
+    low = jnp.sum(lr2_recv[...].astype(F32), axis=0).astype(BF16).astype(F32)
     ranks = jnp.broadcast_to(low.reshape(group // per, 1, LANES), (group // per, per, LANES)).reshape(group, LANES)
     ranks = jnp.where(turn, ranks, 0.0).astype(BF16)
-    ranks = jnp.dot(ranks, fold, preferred_element_type=F32) * keep_ref[...]
+    ranks = jnp.dot(ranks, fold, preferred_element_type=F32) * keep_ref[c]
     ranks = ranks.T.astype(BF16)
     tag = tag_t[...]
     corr = jnp.zeros((LANES, group), F32)
@@ -392,8 +432,19 @@
     for i in range(line):
         mix(i)
 
-    for cp in (all_x, all_comb, all_col, all_disp, all_lr1, all_lr2, all_cor, all_ret):
+    for cp in (all_x, all_comb, all_disp, all_lr2, all_cor, all_ret):
         cp.wait_send()
+
+    @pl.when(c == 1)
+    def _():
+        some_col.wait_send()
+        some_lr1.wait_send()
+        all_lr1.wait_send()
+
+    @pl.when(c == 0)
+    def _():
+        all_col.wait_send()
+
     adn_copy.wait_send()
     aup_copy.wait_send()
     for i in range(line):
@@ -406,10 +457,7 @@
 
         out_ref[:, j * wide_n : (j + 1) * wide_n] = lax.fori_loop(0, line - 1, add, own_part[j]).astype(BF16)
 
-    out_copy = pltpu.make_async_copy(out_ref, out_hbm, out_sem.at[0])
-    out_copy.start()
     all_part.wait_send()
-    out_copy.wait()
 
 
 def per_device(tokens, idx, gates, aid, wg, wu, wd, adn, aup):
@@ -435,32 +483,31 @@
     hbm = pl.BlockSpec(memory_space=pl.ANY)
     return pl.pallas_call(
         functools.partial(kernel, line, plane, cap, top),
-        out_shape=jax.ShapeDtypeStruct((rows, width), BF16),
+        out_shape=pltpu.VMEM((rows, width), BF16),
         in_specs=[hbm] * 9,
-        out_specs=hbm,
+        out_specs=pl.BlockSpec(memory_space=pltpu.VMEM),
         scratch_shapes=[
-            blocks(rows, width), pltpu.VMEM((top, rows), jnp.int32), full(top, rows), pltpu.VMEM((1, aid.shape[0]), jnp.int32),
+            pltpu.VMEM((top, rows), jnp.int32), full(top, rows), pltpu.VMEM((1, aid.shape[0]), jnp.int32),
             blocks(half, width), blocks(half, width), blocks(half, width),
             blocks(LANES, bank), blocks(LANES, bank),
             blocks(line, rows, width), blocks(line, rows, LANES), blocks(line, rows, LANES),
             blocks(line, plane * cap, rows),
-            blocks(plane, line, rows, LANES),
+            blocks(2, plane, line, rows, LANES),
             blocks(plane, line, cap, width), blocks(plane, line, cap, width), blocks(plane, line, cap, width),
             blocks(2 * slots, width), full(half, 2 * slots), full(half, 2 * slots), blocks(2 * slots, half),
-            full(line, slots, wide_n),
             blocks(line, plane, line, cap, wide_n), blocks(line, plane, line, cap, wide_n),
-            blocks(group, LANES), blocks(LANES, group), full(group, LANES),
-            full(short, LANES), full(plane, short, LANES), full(short, LANES), full(line, short, LANES),
+            blocks(2, group, LANES), blocks(LANES, group), full(2, group, LANES),
+            blocks(2, short, LANES), blocks(plane, short, LANES), blocks(short, LANES), blocks(line, short, LANES),
             blocks(plane, line, rows, LANES), blocks(plane, line, rows, LANES),
             blocks(line, plane, line, cap, wide_n), blocks(line, plane, line, cap, wide_n),
             blocks(line, line, rows, wide_n), blocks(line, line, rows, wide_n), full(line, rows, wide_n),
-            sems(4), sems(1), sems(3), sems(2), sems(2), sems(2),
-            sems(1), sems(line * line), sems(1), sems(line), sems(1), sems(1), sems(1), sems(line), sems(line), sems(line),
-            sems(1), sems(1), sems(1), sems(1), sems(1), sems(1), sems(1), sems(line), sems(1), sems(1),
+            sems(4), sems(3), sems(2), sems(2), sems(2),
+            sems(1), sems(line * line), sems(1), sems(line), sems(1), sems(2), sems(1), sems(line), sems(line), sems(line),
+            sems(2), sems(1), sems(1), sems(1), sems(1), sems(1), sems(1), sems(line), sems(1), sems(1),
             sems(line), sems(line),
         ],
         compiler_params=pltpu.CompilerParams(
-            collective_id=0, has_side_effects=True, vmem_limit_bytes=60 * 1024 * 1024
+            collective_id=0, has_side_effects=True, vmem_limit_bytes=62 * 1024 * 1024
         ),
     )(tokens, idx.T, gates.T, aid.reshape(1, -1), wg.swapaxes(1, 2), wu.swapaxes(1, 2), wd, adn, aup)
 

time: 36.7 us -> 34.8 us (0.948)
  Pallas kernels: 35 us -> 34 us
  local copies, waits for them, and re-layouts: 1.47 us -> 0.63 us
    pallas_call x1, Pallas kernels: 35 us -> 34 us  [per_device(): pl.pallas_call(functools.partial(kernel, line, plane, cap, top), out_shap...]
    unnamed x1, local copies, waits for them, and re-layouts: 1.47 us -> 0.63 us
where the time goes in v3:
time: 34.8 us; the launch traced here: 34.7 us
  Pallas kernels  34 us (98%)
  local copies, waits for them, and re-layouts  0.63 us (2%)
    pallas_call x1, Pallas kernels, per_device(): pl.pallas_call(functools.partial(kernel, line, plane, cap, top), out_shap...  34 us

profile of v3, /device:TPU:0, one launch (start us, length us, event | category | flops | bytes accessed | tf_op | source)
XLA Modules:
  0.0 34.7 jit_solution(10756181703153767117)
XLA Ops:
  0.0 34.0 %shard_map.91 = bf16[16,2048]{1,0:T(8,128)(2,1)S(1)} custom-call(bf16[16,2048]{1,0:T(8,128)(2,1)} %x_hbm.1, s32[6,16]{1,0:T(8,128)} %bitcast.7, f32[6,16]{1,0:T(8,128)} %bitcast.8, s32[1,512]{1,0:T(1,128)} %bitcast.9, bf16[1,704,2048]{2,1,0:T(8,128)(2,1)} %bitcast.5, bf16[1,704,2048]{2,1,0:T(8,128)(2,1)} %bitcast.6, bf16[1,704,2048]{2,1,0:T(8,128)(2,1)} %wd_hbm.1, ...), custom_call_target="tpu_custom_call" | custom-call | tf_op jit(solution)/shard_map/pallas_call | solution.py:484
  34.0 0.6 %copy.11 = bf16[16,2048]{1,0:T(8,128)(2,1)} copy(bf16[16,2048]{1,0:T(8,128)(2,1)S(1)} %shard_map.91) | data formatting | bytes 131072

commit v4 on v3

--- a/solution.py
+++ b/solution.py
@@ -235,7 +235,7 @@
             col_copy(g, s).start()
 
     def take_pick(s):
-        pick = jnp.where(line_comb[s].astype(F32) > 0.0, 1.0, 0.0).T[:block]
+        pick = jnp.where(line_comb[s].astype(F32) != 0.0, 1.0, 0.0).T[:block]
         pick_ref[pl.ds(s, 1)] = pick.astype(BF16).reshape(1, block, rows)
 
     def pack(s, k):
@@ -337,25 +337,27 @@
     local[0].wait()
     adn_copy.wait_recv()
 
+    @pl.when(c == 0)
+    def _():
+        receive(0)
+        for k in range(1, line):
+            receive(k)
+            multiply(k - 1)
+        multiply(line - 1)
+
     @pl.when(c == 1)
     def _():
         some_col.wait_recv()
         down(1)
         lr1_recv[pl.ds(g, 1)] = lr_send[1].reshape(1, group // per, LANES)
-
-    for k in range(line // 2):
-        receive(k)
-    for k in range(line // 2, line):
-        receive(k)
-    @pl.when(c == 1)
-    def _():
+        for k in range(line):
+            receive(k)
         all_col.wait_recv()
         down(0)
         lr1_copy(0, g).start()
-
-    for k in range(line - 1):
-        multiply(k)
-    multiply(line - 1)
+        for k in range(line):
+            multiply(k)
+
     local[4].wait()
 
     def down_sib(i):

time: 34.8 us -> 34.5 us (level)
  no operation moved by 1% of the time
where the time goes in v4:
time: 34.5 us; the launch traced here: 34.3 us
  Pallas kernels  33.7 us (98%)
  local copies, waits for them, and re-layouts  0.63 us (2%)
    pallas_call x1, Pallas kernels, per_device(): pl.pallas_call(functools.partial(kernel, line, plane, cap, top), out_shap...  33.7 us

profile of v4, /device:TPU:0, one launch (start us, length us, event | category | flops | bytes accessed | tf_op | source)
XLA Modules:
  0.0 34.3 jit_solution(18230159386443414643)
XLA Ops:
  0.0 33.7 %shard_map.91 = bf16[16,2048]{1,0:T(8,128)(2,1)S(1)} custom-call(bf16[16,2048]{1,0:T(8,128)(2,1)} %x_hbm.1, s32[6,16]{1,0:T(8,128)} %bitcast.7, f32[6,16]{1,0:T(8,128)} %bitcast.8, s32[1,512]{1,0:T(1,128)} %bitcast.9, bf16[1,704,2048]{2,1,0:T(8,128)(2,1)} %bitcast.5, bf16[1,704,2048]{2,1,0:T(8,128)(2,1)} %bitcast.6, bf16[1,704,2048]{2,1,0:T(8,128)(2,1)} %wd_hbm.1, ...), custom_call_target="tpu_custom_call" | custom-call | tf_op jit(solution)/shard_map/pallas_call | solution.py:486
  33.7 0.6 %copy.11 = bf16[16,2048]{1,0:T(8,128)(2,1)} copy(bf16[16,2048]{1,0:T(8,128)(2,1)S(1)} %shard_map.91) | data formatting | bytes 131072

commit v5 on v4

--- a/solution.py
+++ b/solution.py
@@ -314,10 +314,14 @@
     def masked(v, t, k):
         return jnp.where(t == jnp.asarray(k, BF16), v, jnp.zeros_like(v))
 
-    fi = lax.broadcasted_iota(jnp.int32, (LANES, LANES), 0)
-    fj = lax.broadcasted_iota(jnp.int32, (LANES, LANES), 1)
-    fold = jnp.where(lax.rem(fi, RANK) == lax.rem(fj, RANK), 1.0, 0.0).astype(BF16)
-    turn = lax.div(lane_g, RANK) == lax.rem(lax.broadcasted_iota(jnp.int32, (group, LANES), 0), per)
+    def fold_turn():
+        fi = lax.broadcasted_iota(jnp.int32, (LANES, LANES), 0)
+        fj = lax.broadcasted_iota(jnp.int32, (LANES, LANES), 1)
+        fold = jnp.where(lax.rem(fi, RANK) == lax.rem(fj, RANK), 1.0, 0.0).astype(BF16)
+        lane = lax.broadcasted_iota(jnp.int32, (group, LANES), 1)
+        row = lax.broadcasted_iota(jnp.int32, (group, LANES), 0)
+        return fold, lax.div(lane, RANK) == lax.rem(row, per)
+
 
     def down(par):
         cols = col[par].reshape(group, LANES)
@@ -329,6 +333,7 @@
                 [adn[:, k * LANES : (k + 1) * LANES], adn[:, (k + 1) * LANES : (k + 2) * LANES]], axis=0
             )
             terms = terms + jnp.dot(wide, tall, preferred_element_type=F32)
+        fold, turn = fold_turn()
         terms = (terms * keep_ref[par]).astype(BF16)
         folded = jnp.where(turn, jnp.dot(terms, fold, preferred_element_type=F32), 0.0)
         lr_send[par] = jnp.sum(folded.reshape(group // per, per, LANES), axis=1).astype(BF16)
@@ -374,25 +379,37 @@
         ret_recv[i, pl.ds(g, 1)] = ret_send[i, pl.ds(g, 1)]
         plane_peers(lambda d: ret_copy(i, d, g).start())
 
-    for i in range(line):
-        down_sib(i)
+    def low_sum():
+        lr2_send[...] = jnp.sum(lr1_recv[...].astype(F32), axis=0).astype(BF16)
+        lr2_recv[pl.ds(z, 1)] = lr2_send[...].reshape(1, group // per, LANES)
+        line_far(lambda d: lr2_copy(d, z).start())
+
+    @pl.when(c == 0)
+    def _():
+        for i in range(line):
+            down_sib(i)
+        all_lr1.wait_recv()
+        low_sum()
+        for i in range(line):
+            finish(i)
+
     @pl.when(c == 1)
     def _():
+        down_sib(0)
+        finish(0)
+        down_sib(1)
         some_lr1.wait_recv()
-
-    @pl.when(c == 0)
-    def _():
-        all_lr1.wait_recv()
-
-    lr2_send[...] = jnp.sum(lr1_recv[...].astype(F32), axis=0).astype(BF16)
-    lr2_recv[pl.ds(z, 1)] = lr2_send[...].reshape(1, group // per, LANES)
-    line_far(lambda d: lr2_copy(d, z).start())
-    for i in range(line):
-        finish(i)
+        low_sum()
+        finish(1)
+        for i in range(2, line):
+            down_sib(i)
+        for i in range(2, line):
+            finish(i)
 
     all_lr2.wait_recv()
     local[3].wait()
     aup_copy.wait_recv()
+    fold, turn = fold_turn()
     low = jnp.sum(lr2_recv[...].astype(F32), axis=0).astype(BF16).astype(F32)
     ranks = jnp.broadcast_to(low.reshape(group // per, 1, LANES), (group // per, per, LANES)).reshape(group, LANES)
     ranks = jnp.where(turn, ranks, 0.0).astype(BF16)

time: 34.5 us -> 33.5 us (0.971)
  Pallas kernels: 33.7 us -> 32.7 us
    pallas_call x1, Pallas kernels: 33.7 us -> 32.7 us  [per_device(): pl.pallas_call(functools.partial(kernel, line, plane, cap, top), out_shap...]
where the time goes in v5:
time: 33.5 us; the launch traced here: 33.4 us
  Pallas kernels  32.7 us (98%)
  local copies, waits for them, and re-layouts  0.63 us (2%)
    pallas_call x1, Pallas kernels, per_device(): pl.pallas_call(functools.partial(kernel, line, plane, cap, top), out_shap...  32.7 us

profile of v5, /device:TPU:0, one launch (start us, length us, event | category | flops | bytes accessed | tf_op | source)
XLA Modules:
  0.0 33.4 jit_solution(5792893760725996049)
XLA Ops:
  0.0 32.7 %shard_map.91 = bf16[16,2048]{1,0:T(8,128)(2,1)S(1)} custom-call(bf16[16,2048]{1,0:T(8,128)(2,1)} %x_hbm.1, s32[6,16]{1,0:T(8,128)} %bitcast.7, f32[6,16]{1,0:T(8,128)} %bitcast.8, s32[1,512]{1,0:T(1,128)} %bitcast.9, bf16[1,704,2048]{2,1,0:T(8,128)(2,1)} %bitcast.5, bf16[1,704,2048]{2,1,0:T(8,128)(2,1)} %bitcast.6, bf16[1,704,2048]{2,1,0:T(8,128)(2,1)} %wd_hbm.1, ...), custom_call_target="tpu_custom_call" | custom-call | tf_op jit(solution)/shard_map/pallas_call | solution.py:503
  32.7 0.6 %copy.11 = bf16[16,2048]{1,0:T(8,128)(2,1)} copy(bf16[16,2048]{1,0:T(8,128)(2,1)S(1)} %shard_map.91) | data formatting | bytes 131072
